TPU v7x, 256 devices: a whole 4x4x8 slice. The times are simulated.
256 devices in a mesh: gx: 8 (over x, z_lo), gy: 8 (over z_hi, core), gz: 4 (over y).
Axes of the slice: x: 4, y: 4, z: 8 (z_hi: 4, z_lo: 2; z = z_hi * 2 + z_lo), core: 2. Of those that a mesh axis runs over, the one named last changes fastest.
Arguments:
- partials: float32 [32, 128, 128, 512], P('gx', None, 'gy', 'gz'), may hold values from -40 to 40
- code_bits: int32 [32, 128], replicated, may hold values from 0 to 1
- group_map: int32 [32], replicated, may hold values from 0 to 31, each once
- velocity: float32 [128, 128, 512], P('gx', 'gy', 'gz'), may hold values from 1.5 to 4.5
Outputs:
- gradient: float32 [128, 128, 512], P('gx', 'gy', 'gz')
- new_model: float32 [128, 128, 512], P('gx', 'gy', 'gz')
Inputs may be any that keep to these rules, and one draw needn't show every extreme that they name: `group_map`: every group of 0 to 31 stands in exactly one slot.
All inputs are finite; a program needn't handle non-finite values.
Results may differ from a plain program's by a relative error of at most 0.0001.
Values sent between devices are 32-bit elements; how exact they have to be, the bound alone decides.
A program may use at most 64 MiB of HBM per device.

v0:
```python
import functools

import jax
import jax.numpy as jnp
from jax import lax
from jax.sharding import Mesh
from jax.sharding import PartitionSpec as P

ITERS = 3
GX = ("gx_0", "gx_1")
GY = ("gy_0", "gy_1")
GX_GY_GZ = ("gx_0", "gx_1", "gy_0", "gy_1", "gz")


step_length = 0.5
tv_weight = 0.2
dual_step = 0.28
primal_step = 0.28


def from_behind(block, axis, distance):
    devices = range(lax.axis_size(axis))
    route = [(i - distance, i) for i in devices if i - distance in devices]
    return lax.ppermute(block, axis, route)


def over_axes(shard, axes):
    return functools.reduce(lax.psum, axes, shard)


def edge_mask(position, count, length, shape):
    global_index = position * length + jnp.arange(length, dtype=jnp.int32)
    keep = (global_index < count * length - 1).astype(jnp.float32)
    return keep.reshape(shape)


def neighbours_after(extra):
    next_x = jnp.concatenate([extra[1:], from_behind(extra[:1], GX, -1)], 0)
    next_y = jnp.concatenate([extra[:, 1:], from_behind(extra[:, :1], GY, -1)], 1)
    next_z = jnp.concatenate([extra[:, :, 1:], from_behind(extra[:, :, :1], "gz", -1)], 2)
    return (next_x, next_y, next_z)


def neighbours_before(dual_field):
    before_x = jnp.concatenate([from_behind(dual_field[0, -1:], GX, 1), dual_field[0, :-1]], 0)
    before_y = jnp.concatenate(
        [from_behind(dual_field[1, :, -1:], GY, 1), dual_field[1, :, :-1]], 1
    )
    before_z = jnp.concatenate(
        [from_behind(dual_field[2, :, :, -1:], "gz", 1), dual_field[2, :, :, :-1]], 2
    )
    return (before_x, before_y, before_z)


def shards(partials, code_bits, group_map, velocity):
    groups = group_map.shape[0]
    block_x, block_y, block_z = velocity.shape
    onehot = (group_map[:, None] == jnp.arange(groups, dtype=jnp.int32)[None, :]).astype(
        jnp.float32
    )
    slot_bits = jnp.dot(onehot, code_bits.astype(jnp.float32), precision=lax.Precision.HIGHEST)
    sign_table = 2.0 * slot_bits - 1.0
    local_signs = lax.dynamic_slice_in_dim(sign_table, lax.axis_index(GX) * block_x, block_x, 1)
    gradient = jnp.einsum(
        "gx,gxyz->xyz",
        local_signs,
        lax.all_to_all(partials, GX, split_axis=1, concat_axis=0, tiled=True),
        precision=lax.Precision.HIGHEST,
    )
    square_sum = over_axes(jnp.sum(gradient * gradient), GX_GY_GZ)
    cell_count = (
        block_x * block_y * block_z * lax.axis_size(GX) * lax.axis_size(GY) * lax.axis_size("gz")
    )
    step_scale = step_length / jnp.sqrt(square_sum / cell_count + 1.0)
    target = velocity - step_scale * gradient
    mask_x = edge_mask(lax.axis_index(GX), lax.axis_size(GX), block_x, (block_x, 1, 1))
    mask_y = edge_mask(lax.axis_index(GY), lax.axis_size(GY), block_y, (1, block_y, 1))
    mask_z = edge_mask(lax.axis_index("gz"), lax.axis_size("gz"), block_z, (1, 1, block_z))
    current = target
    extra = target
    dual_field = jnp.zeros((3,) + target.shape, jnp.float32)
    for iteration in range(ITERS):
        next_x, next_y, next_z = neighbours_after(extra)
        differences = jnp.stack(
            [(next_x - extra) * mask_x, (next_y - extra) * mask_y, (next_z - extra) * mask_z]
        )
        dual_field = dual_field + dual_step * differences
        magnitude = jnp.sqrt(jnp.sum(dual_field * dual_field, axis=0))
        dual_field = dual_field / jnp.maximum(1.0, magnitude / tv_weight)[None]
        before_x, before_y, before_z = neighbours_before(dual_field)
        spread = dual_field[0] - before_x + (dual_field[1] - before_y) + (dual_field[2] - before_z)
        updated = (current + primal_step * spread + primal_step * target) / (1.0 + primal_step)
        extra = 2.0 * updated - current
        current = updated
    return (gradient, current)


def solution(mesh):
    torus = Mesh(
        mesh.devices.reshape(4, 2, 4, 2, mesh.shape["gz"]), ("gx_0", "gx_1", "gy_0", "gy_1", "gz")
    )
    placed = (P(GX, None, GY, "gz"), P(), P(), P(GX, GY, "gz"))
    return jax.shard_map(
        shards,
        mesh=torus,
        in_specs=placed,
        out_specs=(P(GX, GY, "gz"), P(GX, GY, "gz")),
        check_vma=False,
    )
```

profile of v0, /device:TPU:1, one launch (start us, length us, event | category | flops | bytes accessed | tf_op | source)
XLA Modules:
  0.0 183.8 jit_solution(953719524343635851)
XLA Ops:
  0.6 4.8 %copy.34 = f32[4,128,16,128]{3,2,0,1:T(8,128)} copy(f32[4,128,16,128]{3,2,1,0:T(8,128)} %param.4) | data formatting | bytes 8388608 | tf_op args[0]
  5.4 6.3 %all-to-all-start = ((f32[4,128,16,128]{3,2,0,1:T(8,128)}), f32[4,128,16,128]{3,2,0,1:T(8,128)}, u32[]{:S(2)}, u32[]{:S(2)}) async-start(f32[4,128,16,128]{3,2,0,1:T(8,128)} %copy.34), calls=%async_computation | async-start | bytes 8388608 | tf_op jit(solution)/shard_map/all_to_all | solution.py:67
  12.1 47.9 %all-to-all-done = f32[4,128,16,128]{3,2,0,1:T(8,128)} async-done(((f32[4,128,16,128]{3,2,0,1:T(8,128)}), f32[4,128,16,128]{3,2,0,1:T(8,128)}, u32[]{:S(2)}, u32[]{:S(2)}) %all-to-all-start) | async-done | bytes 4194336 | tf_op jit(solution)/shard_map/all_to_all | solution.py:67
  59.9 2.8 %copy.36 = f32[8,4,16,16,128]{4,3,2,1,0:T(8,128)S(1)} copy(f32[8,4,16,16,128]{4,3,1,2,0:T(8,128)} %bitcast.4) | data formatting | bytes 8388608 | tf_op jit(solution)/shard_map/all_to_all | solution.py:67
  62.7 4.3 %fusion = f32[16,1,16,128]{3,1,2,0:T(1,128)S(1)} fusion(f32[32,16,1,1]{0,2,3,1:T(1,128)S(1)} %bitcast.169, f32[32,16,16,128]{3,2,1,0:T(8,128)S(1)} %bitcast.164), kind=kOutput, calls=%fused_computation | convolution fusion | flops 12582912 | bytes 4327424 | tf_op jit(solution)/shard_map/gx,gxyz->xyz/dot_general | solution.py:64
  67.7 7.8 %psum.35 = f32[]{:T(128)} all-reduce(f32[]{:T(128)} %fusion.48), channel_id=1, replica_groups=mesh['gx_0'=4,'gx_1'=2,'gy_0'=4,'gy_1'=2,'gz'=4] {'gx_0'}, use_global_device_ids=true, to_apply=%region_1.0 | all-reduce | flops 1 | bytes 8 | tf_op jit(solution)/shard_map/psum | solution.py:28
  75.5 5.0 %psum.36 = f32[]{:T(128)} all-reduce(f32[]{:T(128)} %psum.35), channel_id=1, replica_groups=mesh['gx_0'=4,'gx_1'=2,'gy_0'=4,'gy_1'=2,'gz'=4] {'gx_1'}, use_global_device_ids=true, to_apply=%region_2.0 | all-reduce | flops 1 | bytes 8 | tf_op jit(solution)/shard_map/psum | solution.py:28
  80.5 12.6 %psum.37 = f32[]{:T(128)} all-reduce(f32[]{:T(128)} %psum.36), channel_id=1, replica_groups=mesh['gx_0'=4,'gx_1'=2,'gy_0'=4,'gy_1'=2,'gz'=4] {'gy_0'}, use_global_device_ids=true, to_apply=%region_3.0 | all-reduce | flops 1 | bytes 8 | tf_op jit(solution)/shard_map/psum | solution.py:28
  93.1 9.7 %psum.38 = f32[]{:T(128)} all-reduce(f32[]{:T(128)} %psum.37), channel_id=1, replica_groups=mesh['gx_0'=4,'gx_1'=2,'gy_0'=4,'gy_1'=2,'gz'=4] {'gy_1'}, use_global_device_ids=true, to_apply=%region_4.0 | all-reduce | flops 1 | bytes 8 | tf_op jit(solution)/shard_map/psum | solution.py:28
  102.8 9.3 %psum.39 = f32[]{:T(128)} all-reduce(f32[]{:T(128)} %psum.38), channel_id=1, replica_groups=mesh['gx_0'=4,'gx_1'=2,'gy_0'=4,'gy_1'=2,'gz'=4] {'gz'}, use_global_device_ids=true, to_apply=%region_5.0 | all-reduce | flops 1 | bytes 8 | tf_op jit(solution)/shard_map/psum | solution.py:28
  115.5 4.3 %collective-permute-start.1 = (f32[16,1,128]{2,0,1:T(8,128)S(1)}, f32[16,1,128]{2,0,1:T(8,128)S(1)}, u32[]{:S(2)}, u32[]{:S(2)}) collective-permute-start(f32[16,1,128]{2,0,1:T(8,128)S(1)} %slice.183), channel_id=1, source_target_pairs={{4,0},{8,4},{12,8},{16,12},{20,16},{24,20},{28,24},{5,1},{9,5},{13... | collective-permute-start | bytes 24584 | tf_op jit(solution)/shard_map/ppermute | solution.py:24
  122.2 4.0 %collective-permute-start.5 = (f32[16,16,1]{2,0,1:T(8,128)S(1)}, f32[16,16,1]{2,0,1:T(8,128)S(1)}, u32[]{:S(2)}, u32[]{:S(2)}) collective-permute-start(f32[16,16,1]{2,0,1:T(8,128)S(1)} %copy.40), channel_id=1, source_target_pairs={{0,1},{1,2},{2,3},{4,5},{5,6},{6,7},{8,9},{9,10},{10,11},{12,13},{... | collective-permute-start | bytes 3080 | tf_op jit(solution)/shard_map/ppermute | solution.py:24
  126.2 4.1 %collective-permute-start.3 = (f32[1,16,128]{2,0,1:T(1,128)S(1)}, f32[1,16,128]{2,0,1:T(1,128)S(1)}, u32[]{:S(2)}, u32[]{:S(2)}) collective-permute-start(f32[1,16,128]{2,0,1:T(1,128)S(1)} %slice_bitcast_fusion.23), channel_id=1, source_target_pairs={{0,32},{32,64},{64,96},{96,128},{128,160},{160,192},{192,224},{1,3... | collective-permute-start | bytes 24584 | tf_op jit(solution)/shard_map/ppermute | solution.py:24
  130.4 2.5 %collective-permute-start.4 = (f32[16,1,128]{2,0,1:T(8,128)S(1)}, f32[16,1,128]{2,0,1:T(8,128)S(1)}, u32[]{:S(2)}, u32[]{:S(2)}) collective-permute-start(f32[16,1,128]{2,0,1:T(8,128)S(1)} %slice_bitcast_fusion.22), channel_id=1, source_target_pairs={{0,4},{4,8},{8,12},{12,16},{16,20},{20,24},{24,28},{1,5},{5,9},{9,... | collective-permute-start | bytes 24584 | tf_op jit(solution)/shard_map/ppermute | solution.py:24
  135.1 1.9 %collective-permute-start.7 = (f32[16,1,128]{2,0,1:T(8,128)S(1)}, f32[16,1,128]{2,0,1:T(8,128)S(1)}, u32[]{:S(2)}, u32[]{:S(2)}) collective-permute-start(f32[16,1,128]{2,0,1:T(8,128)S(1)} %slice.198), channel_id=1, source_target_pairs={{4,0},{8,4},{12,8},{16,12},{20,16},{24,20},{28,24},{5,1},{9,5},{13... | collective-permute-start | bytes 24584 | tf_op jit(solution)/shard_map/ppermute | solution.py:24
  138.4 5.6 %collective-permute-done.8 = f32[16,16,1]{2,0,1:T(8,128)S(1)} collective-permute-done((f32[16,16,1]{2,0,1:T(8,128)S(1)}, f32[16,16,1]{2,0,1:T(8,128)S(1)}, u32[]{:S(2)}, u32[]{:S(2)}) %collective-permute-start.8) | collective-permute-done | bytes 1056 | tf_op jit(solution)/shard_map/ppermute | solution.py:24
  144.9 2.0 %collective-permute-start.11 = (f32[16,16,1]{2,0,1:T(8,128)S(1)}, f32[16,16,1]{2,0,1:T(8,128)S(1)}, u32[]{:S(2)}, u32[]{:S(2)}) collective-permute-start(f32[16,16,1]{2,0,1:T(8,128)S(1)} %copy.43), channel_id=1, source_target_pairs={{0,1},{1,2},{2,3},{4,5},{5,6},{6,7},{8,9},{9,10},{10,11},{12,13},{... | collective-permute-start | bytes 3080 | tf_op jit(solution)/shard_map/ppermute | solution.py:24
  146.9 5.9 %collective-permute-start.10 = (f32[16,1,128]{2,0,1:T(8,128)S(1)}, f32[16,1,128]{2,0,1:T(8,128)S(1)}, u32[]{:S(2)}, u32[]{:S(2)}) collective-permute-start(f32[16,1,128]{2,0,1:T(8,128)S(1)} %slice_bitcast_fusion.20), channel_id=1, source_target_pairs={{0,4},{4,8},{8,12},{12,16},{16,20},{20,24},{24,28},{1,5},{5,9},{9,... | collective-permute-start | bytes 24584 | tf_op jit(solution)/shard_map/ppermute | solution.py:24
  152.8 4.3 %collective-permute-start.9 = (f32[1,16,128]{2,0,1:T(1,128)S(1)}, f32[1,16,128]{2,0,1:T(1,128)S(1)}, u32[]{:S(2)}, u32[]{:S(2)}) collective-permute-start(f32[1,16,128]{2,0,1:T(1,128)S(1)} %slice_bitcast_fusion.21), channel_id=1, source_target_pairs={{0,32},{32,64},{64,96},{96,128},{128,160},{160,192},{192,224},{1,3... | collective-permute-start | bytes 24584 | tf_op jit(solution)/shard_map/ppermute | solution.py:24
  159.3 1.9 %collective-permute-start.13 = (f32[16,1,128]{2,0,1:T(8,128)S(1)}, f32[16,1,128]{2,0,1:T(8,128)S(1)}, u32[]{:S(2)}, u32[]{:S(2)}) collective-permute-start(f32[16,1,128]{2,0,1:T(8,128)S(1)} %slice.213), channel_id=1, source_target_pairs={{4,0},{8,4},{12,8},{16,12},{20,16},{24,20},{28,24},{5,1},{9,5},{13... | collective-permute-start | bytes 24584 | tf_op jit(solution)/shard_map/ppermute | solution.py:24
  162.7 4.3 %collective-permute-done.14 = f32[16,16,1]{2,0,1:T(8,128)S(1)} collective-permute-done((f32[16,16,1]{2,0,1:T(8,128)S(1)}, f32[16,16,1]{2,0,1:T(8,128)S(1)}, u32[]{:S(2)}, u32[]{:S(2)}) %collective-permute-start.14) | collective-permute-done | bytes 1056 | tf_op jit(solution)/shard_map/ppermute | solution.py:24
  167.9 2.4 %collective-permute-start.17 = (f32[16,16,1]{2,0,1:T(8,128)S(1)}, f32[16,16,1]{2,0,1:T(8,128)S(1)}, u32[]{:S(2)}, u32[]{:S(2)}) collective-permute-start(f32[16,16,1]{2,0,1:T(8,128)S(1)} %copy.46), channel_id=1, source_target_pairs={{0,1},{1,2},{2,3},{4,5},{5,6},{6,7},{8,9},{9,10},{10,11},{12,13},{... | collective-permute-start | bytes 3080 | tf_op jit(solution)/shard_map/ppermute | solution.py:24
  170.4 4.5 %collective-permute-start.15 = (f32[1,16,128]{2,0,1:T(1,128)S(1)}, f32[1,16,128]{2,0,1:T(1,128)S(1)}, u32[]{:S(2)}, u32[]{:S(2)}) collective-permute-start(f32[1,16,128]{2,0,1:T(1,128)S(1)} %slice_bitcast_fusion.19), channel_id=1, source_target_pairs={{0,32},{32,64},{64,96},{96,128},{128,160},{160,192},{192,224},{1,3... | collective-permute-start | bytes 24584 | tf_op jit(solution)/shard_map/ppermute | solution.py:24
  174.9 7.2 %collective-permute-start.16 = (f32[16,1,128]{2,0,1:T(8,128)S(1)}, f32[16,1,128]{2,0,1:T(8,128)S(1)}, u32[]{:S(2)}, u32[]{:S(2)}) collective-permute-start(f32[16,1,128]{2,0,1:T(8,128)S(1)} %slice_bitcast_fusion.18), channel_id=1, source_target_pairs={{0,4},{4,8},{8,12},{12,16},{16,20},{20,24},{24,28},{1,5},{5,9},{9,... | collective-permute-start | bytes 24584 | tf_op jit(solution)/shard_map/ppermute | solution.py:24
  (91 shorter events, 16.4 us)
Async XLA Ops:
  5.4 6.3 %copy-start.2 = (s32[32,128]{1,0:T(8,128)S(1)}, s32[32,128]{1,0:T(8,128)}, u32[]{:S(2)}) copy-start(s32[32,128]{1,0:T(8,128)} %param.5) | copy-start | bytes 49156
  5.4 6.3 %copy-start.3 = (s32[32]{0:T(128)S(1)}, s32[32]{0:T(128)}, u32[]{:S(2)}) copy-start(s32[32]{0:T(128)} %param.6) | copy-start | bytes 388
  5.4 54.5 %all-to-all-start = ((f32[4,128,16,128]{3,2,0,1:T(8,128)}), f32[4,128,16,128]{3,2,0,1:T(8,128)}, u32[]{:S(2)}, u32[]{:S(2)}) async-start(f32[4,128,16,128]{3,2,0,1:T(8,128)} %copy.34), calls=%async_computation | async-start | bytes 8388608 | tf_op jit(solution)/shard_map/all_to_all | solution.py:67
  62.7 50.1 %copy-start.1 = (f32[16,16,128]{2,1,0:T(8,128)S(1)}, f32[16,16,128]{2,1,0:T(8,128)}, u32[]{:S(2)}) copy-start(f32[16,16,128]{2,1,0:T(8,128)} %param.7) | copy-start | bytes 393220
  67.1 77.1 %copy-start = (f32[16,1,16,128]{3,1,2,0:T(1,128)}, f32[16,1,16,128]{3,1,2,0:T(1,128)S(1)}, u32[]{:S(2)}) copy-start(f32[16,1,16,128]{3,1,2,0:T(1,128)S(1)} %fusion) | copy-start | bytes 393220
  112.9 7.0 %collective-permute-start.2 = (f32[16,16,1]{2,0,1:T(8,128)S(1)}, f32[16,16,1]{2,0,1:T(8,128)S(1)}, u32[]{:S(2)}, u32[]{:S(2)}) collective-permute-start(f32[16,16,1]{2,0,1:T(8,128)S(1)} %bitcast.165), channel_id=1, source_target_pairs={{1,0},{2,1},{3,2},{5,4},{6,5},{7,6},{9,8},{10,9},{11,10},{13,12},{... | collective-permute-start | bytes 3080 | tf_op jit(solution)/shard_map/ppermute | solution.py:24
  114.2 5.7 %collective-permute-start = (f32[1,16,128]{2,0,1:T(1,128)S(1)}, f32[1,16,128]{2,0,1:T(1,128)S(1)}, u32[]{:S(2)}, u32[]{:S(2)}) collective-permute-start(f32[1,16,128]{2,0,1:T(1,128)S(1)} %slice.181), channel_id=1, source_target_pairs={{32,0},{64,32},{96,64},{128,96},{160,128},{192,160},{224,192},{33,... | collective-permute-start | bytes 24584 | tf_op jit(solution)/shard_map/ppermute | solution.py:24
  115.5 5.9 %collective-permute-start.1 = (f32[16,1,128]{2,0,1:T(8,128)S(1)}, f32[16,1,128]{2,0,1:T(8,128)S(1)}, u32[]{:S(2)}, u32[]{:S(2)}) collective-permute-start(f32[16,1,128]{2,0,1:T(8,128)S(1)} %slice.183), channel_id=1, source_target_pairs={{4,0},{8,4},{12,8},{16,12},{20,16},{24,20},{28,24},{5,1},{9,5},{13... | collective-permute-start | bytes 24584 | tf_op jit(solution)/shard_map/ppermute | solution.py:24
  122.2 10.7 %collective-permute-start.5 = (f32[16,16,1]{2,0,1:T(8,128)S(1)}, f32[16,16,1]{2,0,1:T(8,128)S(1)}, u32[]{:S(2)}, u32[]{:S(2)}) collective-permute-start(f32[16,16,1]{2,0,1:T(8,128)S(1)} %copy.40), channel_id=1, source_target_pairs={{0,1},{1,2},{2,3},{4,5},{5,6},{6,7},{8,9},{9,10},{10,11},{12,13},{... | collective-permute-start | bytes 3080 | tf_op jit(solution)/shard_map/ppermute | solution.py:24
  126.2 6.7 %collective-permute-start.3 = (f32[1,16,128]{2,0,1:T(1,128)S(1)}, f32[1,16,128]{2,0,1:T(1,128)S(1)}, u32[]{:S(2)}, u32[]{:S(2)}) collective-permute-start(f32[1,16,128]{2,0,1:T(1,128)S(1)} %slice_bitcast_fusion.23), channel_id=1, source_target_pairs={{0,32},{32,64},{64,96},{96,128},{128,160},{160,192},{192,224},{1,3... | collective-permute-start | bytes 24584 | tf_op jit(solution)/shard_map/ppermute | solution.py:24
  130.4 3.3 %collective-permute-start.4 = (f32[16,1,128]{2,0,1:T(8,128)S(1)}, f32[16,1,128]{2,0,1:T(8,128)S(1)}, u32[]{:S(2)}, u32[]{:S(2)}) collective-permute-start(f32[16,1,128]{2,0,1:T(8,128)S(1)} %slice_bitcast_fusion.22), channel_id=1, source_target_pairs={{0,4},{4,8},{8,12},{12,16},{16,20},{20,24},{24,28},{1,5},{5,9},{9,... | collective-permute-start | bytes 24584 | tf_op jit(solution)/shard_map/ppermute | solution.py:24
  133.8 10.2 %collective-permute-start.6 = (f32[1,16,128]{2,0,1:T(1,128)S(1)}, f32[1,16,128]{2,0,1:T(1,128)S(1)}, u32[]{:S(2)}, u32[]{:S(2)}) collective-permute-start(f32[1,16,128]{2,0,1:T(1,128)S(1)} %slice.196), channel_id=1, source_target_pairs={{32,0},{64,32},{96,64},{128,96},{160,128},{192,160},{224,192},{33,... | collective-permute-start | bytes 24584 | tf_op jit(solution)/shard_map/ppermute | solution.py:24
  135.1 8.9 %collective-permute-start.7 = (f32[16,1,128]{2,0,1:T(8,128)S(1)}, f32[16,1,128]{2,0,1:T(8,128)S(1)}, u32[]{:S(2)}, u32[]{:S(2)}) collective-permute-start(f32[16,1,128]{2,0,1:T(8,128)S(1)} %slice.198), channel_id=1, source_target_pairs={{4,0},{8,4},{12,8},{16,12},{20,16},{24,20},{28,24},{5,1},{9,5},{13... | collective-permute-start | bytes 24584 | tf_op jit(solution)/shard_map/ppermute | solution.py:24
  137.0 7.0 %collective-permute-start.8 = (f32[16,16,1]{2,0,1:T(8,128)S(1)}, f32[16,16,1]{2,0,1:T(8,128)S(1)}, u32[]{:S(2)}, u32[]{:S(2)}) collective-permute-start(f32[16,16,1]{2,0,1:T(8,128)S(1)} %bitcast.166), channel_id=1, source_target_pairs={{1,0},{2,1},{3,2},{5,4},{6,5},{7,6},{9,8},{10,9},{11,10},{13,12},{... | collective-permute-start | bytes 3080 | tf_op jit(solution)/shard_map/ppermute | solution.py:24
  144.9 12.2 %collective-permute-start.11 = (f32[16,16,1]{2,0,1:T(8,128)S(1)}, f32[16,16,1]{2,0,1:T(8,128)S(1)}, u32[]{:S(2)}, u32[]{:S(2)}) collective-permute-start(f32[16,16,1]{2,0,1:T(8,128)S(1)} %copy.43), channel_id=1, source_target_pairs={{0,1},{1,2},{2,3},{4,5},{5,6},{6,7},{8,9},{9,10},{10,11},{12,13},{... | collective-permute-start | bytes 3080 | tf_op jit(solution)/shard_map/ppermute | solution.py:24
  146.9 10.2 %collective-permute-start.10 = (f32[16,1,128]{2,0,1:T(8,128)S(1)}, f32[16,1,128]{2,0,1:T(8,128)S(1)}, u32[]{:S(2)}, u32[]{:S(2)}) collective-permute-start(f32[16,1,128]{2,0,1:T(8,128)S(1)} %slice_bitcast_fusion.20), channel_id=1, source_target_pairs={{0,4},{4,8},{8,12},{12,16},{16,20},{20,24},{24,28},{1,5},{5,9},{9,... | collective-permute-start | bytes 24584 | tf_op jit(solution)/shard_map/ppermute | solution.py:24
  152.8 5.0 %collective-permute-start.9 = (f32[1,16,128]{2,0,1:T(1,128)S(1)}, f32[1,16,128]{2,0,1:T(1,128)S(1)}, u32[]{:S(2)}, u32[]{:S(2)}) collective-permute-start(f32[1,16,128]{2,0,1:T(1,128)S(1)} %slice_bitcast_fusion.21), channel_id=1, source_target_pairs={{0,32},{32,64},{64,96},{96,128},{128,160},{160,192},{192,224},{1,3... | collective-permute-start | bytes 24584 | tf_op jit(solution)/shard_map/ppermute | solution.py:24
  158.0 8.9 %collective-permute-start.12 = (f32[1,16,128]{2,0,1:T(1,128)S(1)}, f32[1,16,128]{2,0,1:T(1,128)S(1)}, u32[]{:S(2)}, u32[]{:S(2)}) collective-permute-start(f32[1,16,128]{2,0,1:T(1,128)S(1)} %slice.211), channel_id=1, source_target_pairs={{32,0},{64,32},{96,64},{128,96},{160,128},{192,160},{224,192},{33,... | collective-permute-start | bytes 24584 | tf_op jit(solution)/shard_map/ppermute | solution.py:24
  159.3 7.6 %collective-permute-start.13 = (f32[16,1,128]{2,0,1:T(8,128)S(1)}, f32[16,1,128]{2,0,1:T(8,128)S(1)}, u32[]{:S(2)}, u32[]{:S(2)}) collective-permute-start(f32[16,1,128]{2,0,1:T(8,128)S(1)} %slice.213), channel_id=1, source_target_pairs={{4,0},{8,4},{12,8},{16,12},{20,16},{24,20},{28,24},{5,1},{9,5},{13... | collective-permute-start | bytes 24584 | tf_op jit(solution)/shard_map/ppermute | solution.py:24
  161.2 5.7 %collective-permute-start.14 = (f32[16,16,1]{2,0,1:T(8,128)S(1)}, f32[16,16,1]{2,0,1:T(8,128)S(1)}, u32[]{:S(2)}, u32[]{:S(2)}) collective-permute-start(f32[16,16,1]{2,0,1:T(8,128)S(1)} %bitcast.167), channel_id=1, source_target_pairs={{1,0},{2,1},{3,2},{5,4},{6,5},{7,6},{9,8},{10,9},{11,10},{13,12},{... | collective-permute-start | bytes 3080 | tf_op jit(solution)/shard_map/ppermute | solution.py:24
  167.9 14.3 %collective-permute-start.17 = (f32[16,16,1]{2,0,1:T(8,128)S(1)}, f32[16,16,1]{2,0,1:T(8,128)S(1)}, u32[]{:S(2)}, u32[]{:S(2)}) collective-permute-start(f32[16,16,1]{2,0,1:T(8,128)S(1)} %copy.46), channel_id=1, source_target_pairs={{0,1},{1,2},{2,3},{4,5},{5,6},{6,7},{8,9},{9,10},{10,11},{12,13},{... | collective-permute-start | bytes 3080 | tf_op jit(solution)/shard_map/ppermute | solution.py:24
  170.4 11.8 %collective-permute-start.15 = (f32[1,16,128]{2,0,1:T(1,128)S(1)}, f32[1,16,128]{2,0,1:T(1,128)S(1)}, u32[]{:S(2)}, u32[]{:S(2)}) collective-permute-start(f32[1,16,128]{2,0,1:T(1,128)S(1)} %slice_bitcast_fusion.19), channel_id=1, source_target_pairs={{0,32},{32,64},{64,96},{96,128},{128,160},{160,192},{192,224},{1,3... | collective-permute-start | bytes 24584 | tf_op jit(solution)/shard_map/ppermute | solution.py:24
  174.9 8.0 %collective-permute-start.16 = (f32[16,1,128]{2,0,1:T(8,128)S(1)}, f32[16,1,128]{2,0,1:T(8,128)S(1)}, u32[]{:S(2)}, u32[]{:S(2)}) collective-permute-start(f32[16,1,128]{2,0,1:T(8,128)S(1)} %slice_bitcast_fusion.18), channel_id=1, source_target_pairs={{0,4},{4,8},{8,12},{12,16},{16,20},{20,24},{24,28},{1,5},{5,9},{9,... | collective-permute-start | bytes 24584 | tf_op jit(solution)/shard_map/ppermute | solution.py:24
where the time goes:
time: 186 us; the launch traced here: 184 us
  waiting for transfers between devices  61.4 us (33%)
  starting transfers between devices  59.2 us (32%)
  blocking collectives  44.4 us (24%)
  local copies, waits for them, and re-layouts  10.1 us (5%)
  matrix products  4.61 us (2%)
  other arithmetic  2.17 us (1%)
  between operations  1.98 us (1%)
    ppermute x18, starting transfers between devices, from_behind(): return lax.ppermute(block, axis, route)  52.8 us
    all_to_all x1, waiting for transfers between devices, shards(): lax.all_to_all(partials, GX, split_axis=1, concat_axis=0, tiled=True)  47.9 us
    psum x5, blocking collectives, over_axes(): return functools.reduce(lax.psum, axes, shard)  44.4 us
    ppermute x18, waiting for transfers between devices, from_behind(): return lax.ppermute(block, axis, route)  13.5 us
    all_to_all x1, starting transfers between devices, shards(): lax.all_to_all(partials, GX, split_axis=1, concat_axis=0, tiled=True)  6.32 us
    unnamed x10, local copies, waits for them, and re-layouts  5.52 us
    dot_general x1, matrix products, shards(): jnp.einsum('gx,gxyz->xyz', local_signs, lax.all_to_all(partials, GX, spli...  4.35 us
  transfers between devices with their start and end apart: 19, of which 7 were waited for; matrix products, arithmetic and copies ran while one was open for 0% of the time, Pallas kernels for 0%

commit v1 on v0

v1 whole, which is shorter than its diff:
```python
import functools

import jax
import jax.numpy as jnp
from jax import lax
from jax.experimental import pallas as pl
from jax.experimental.pallas import tpu as pltpu
from jax.sharding import PartitionSpec as P

ITERS = 3
HALO = 3
STEP_LENGTH = 0.5
TV_WEIGHT = 0.2
DUAL_STEP = 0.28
PRIMAL_STEP = 0.28
MESH = pl.DeviceIdType.MESH

STREAMS = ((0, 5), (5, 10), (10, 16))
ORDERS = ((0, 1, 2), (1, 2, 0), (2, 0, 1))
HIGH = 5
LOW = 6


def flipped(x, zl, bits):
    bz, bp, bq = bits
    if bz:
        zl = 1 - zl
    if bp:
        x = x + 1 - 2 * (x % 2)
    if bq:
        x = 3 - x
    return x * 2 + zl


def cube_bits(order, idx):
    bits = [0, 0, 0]
    for place, dim in enumerate(order):
        bits[dim] = (idx >> (2 - place)) & 1
    return tuple(bits)


def comm_kernel(
    cells,
    partials, code_bits, group_map, velocity,
    t_out, eh_out, el_out, g_out,
    pin, w, r, xg, xv, packs, landed, ss, a1, a2, bits_s, map_s,
    load_sem, small_sem, rs_send, rs_recv, ar_send, ar_recv,
    h1_send, h1_recv, h2_send, h2_recv,
):
    gx, gy, gz = lax.axis_index("gx"), lax.axis_index("gy"), lax.axis_index("gz")
    x, zl = gx // 2, gx % 2
    zh, core = gy // 2, gy % 2
    z = zh * 2 + zl
    slots = partials.shape[0]
    rows = w.shape[1]

    bits_copy = pltpu.make_async_copy(code_bits, bits_s, small_sem.at[0])
    map_copy = pltpu.make_async_copy(group_map, map_s, small_sem.at[1])
    vel_copy = pltpu.make_async_copy(velocity, xv.at[HALO:HALO + rows, 8:24], small_sem.at[2])
    map_copy.start()
    bits_copy.start()
    loads = {}
    for first in (6, 4, 2, 0):
        for p, (r0, r1) in enumerate(STREAMS):
            for idx in (first + 1, first):
                dest = flipped(x, zl, cube_bits(ORDERS[p], idx))
                span = pl.ds(dest * rows + r0, r1 - r0)
                loads[idx, p] = pltpu.make_async_copy(
                    partials.at[:, span], pin.at[:, span], load_sem.at[p * 8 + idx]
                )
                loads[idx, p].start()
    vel_copy.start()

    flat = [
        (((x + rx) % 4) * 2 + zl, gy, (gz + ry) % 4)
        for rx in range(4) for ry in range(4) if rx or ry
    ]
    tall = []
    for rz in range(8):
        for rc in range(2):
            if rz or rc:
                zz = (z + rz) % 8
                tall.append((x * 2 + zz % 2, (zz // 2) * 2 + (core + rc) % 2, gz))
    gx_up, gx_down = (gx + 1) % 8, (gx + 7) % 8
    gy_up, gy_down = (gy + 1) % 8, (gy + 7) % 8
    diagonal = (gx + 7 + 2 * zl) % 8
    slanted = [(diagonal, gy, gz), (diagonal, gy_up, gz), (diagonal, gy_down, gz)]
    barrier = pltpu.get_barrier_semaphore()
    greeted = flat + tall + slanted
    for peer in greeted:
        pl.semaphore_signal(barrier, inc=1, device_id=peer, device_id_type=MESH)

    def weigh(idx, p):
        r0, r1 = STREAMS[p]
        dest = flipped(x, zl, cube_bits(ORDERS[p], idx))
        loads[idx, p].wait()
        for n in range(r0, r1):
            at = dest * rows + n
            total = None
            for i in range(slots):
                sign = 2.0 * bits_s[map_s[gx * slots + i], at].astype(jnp.float32) - 1.0
                term = sign * pin[i, at]
                total = term if total is None else total + term
            w[idx, n] = total

    def rs_copy(p, hop, src, dst):
        r0, r1 = STREAMS[p]
        place = (0, 0, 1, 1, 2)[hop]
        step = [0, 0, 0]
        step[ORDERS[p][place]] = 1
        return pltpu.make_async_remote_copy(
            src_ref=w.at[src, r0:r1],
            dst_ref=r.at[dst, r0:r1],
            send_sem=rs_send.at[p * 5 + hop],
            recv_sem=rs_recv.at[p * 5 + hop],
            device_id=(flipped(x, zl, step), gy, gz),
            device_id_type=MESH,
        )

    rs = {}
    for p in range(3):
        rs[p, 0] = rs_copy(p, 0, slice(6, 8), slice(2, 4))
        rs[p, 1] = rs_copy(p, 1, slice(4, 6), slice(0, 2))
        rs[p, 2] = rs_copy(p, 2, slice(3, 4), slice(5, 6))
        rs[p, 3] = rs_copy(p, 3, slice(2, 3), slice(4, 5))
        rs[p, 4] = rs_copy(p, 4, slice(1, 2), slice(6, 7))

    map_copy.wait()
    bits_copy.wait()
    for p in range(3):
        weigh(7, p)
        weigh(6, p)
        if p == 0:
            pl.semaphore_wait(barrier, len(greeted))
        rs[p, 0].start()
    for p in range(3):
        weigh(5, p)
        weigh(4, p)
        rs[p, 1].start()
    for p in range(3):
        weigh(3, p)
        weigh(2, p)
    for p in range(3):
        weigh(1, p)
        weigh(0, p)

    def gather_in(p, k, source):
        r0, r1 = STREAMS[p]
        w[k, r0:r1] = w[k, r0:r1] + r[source, r0:r1]

    for p in range(3):
        rs[p, 0].wait_recv()
        gather_in(p, 3, 3)
        rs[p, 2].start()
        gather_in(p, 2, 2)
        rs[p, 3].start()
    for p in range(3):
        rs[p, 1].wait_recv()
        gather_in(p, 1, 1)
        gather_in(p, 0, 0)
    for p in range(3):
        rs[p, 2].wait_recv()
        gather_in(p, 1, 5)
        rs[p, 4].start()

    def halo_copies(block, which):
        down, up = slice(HALO, 2 * HALO), slice(rows, rows + HALO)
        whole, below, above = slice(HALO, HALO + rows), slice(0, HALO), slice(HALO + rows, 2 * HALO + rows)
        first, last, both, under, over = slice(8, 16), slice(16, 24), slice(8, 24), slice(0, 8), slice(24, 32)
        moves = [
            ((gx_up, gy, gz), (up, both), (below, both)),
            ((gx_down, gy, gz), (down, both), (above, both)),
            ((gx, gy_up, gz), (whole, last), (whole, under)),
            ((gx, gy_down, gz), (whole, first), (whole, over)),
            ((gx_up, gy_up, gz), (up, last), (below, under)),
            ((gx_up, gy_down, gz), (up, first), (below, over)),
            ((gx_down, gy_up, gz), (down, last), (above, under)),
            ((gx_down, gy_down, gz), (down, first), (above, over)),
        ]
        return [
            pltpu.make_async_remote_copy(
                src_ref=block.at[src[0], src[1]],
                dst_ref=block.at[dst[0], dst[1]],
                send_sem=h1_send.at[which * 8 + n],
                recv_sem=h1_recv.at[which * 8 + n],
                device_id=peer,
                device_id_type=MESH,
            )
            for n, (peer, src, dst) in enumerate(moves)
        ]

    v_halo = halo_copies(xv, 0)
    g_halo = halo_copies(xg, 1)
    vel_copy.wait()
    for copy in v_halo:
        copy.start()

    square = jnp.zeros((8, 128), jnp.float32)
    for p, (r0, r1) in enumerate(STREAMS):
        rs[p, 3].wait_recv()
        gather_in(p, 0, 4)
    for p, (r0, r1) in enumerate(STREAMS):
        rs[p, 4].wait_recv()
        for n in range(r0, r1):
            value = w[0, n] + r[6, n]
            xg[HALO + n, 8:24] = value
            g_out[n] = value
            value = value * value
            square = square + (value[:8] + value[8:])
    ss[0] = square

    def reduce_copies(src, dst, base, peers):
        return [
            pltpu.make_async_remote_copy(
                src_ref=src,
                dst_ref=dst.at[n],
                send_sem=ar_send.at[base + n],
                recv_sem=ar_recv.at[base + n],
                device_id=peer,
                device_id_type=MESH,
            )
            for n, peer in enumerate(peers)
        ]

    ar1 = reduce_copies(ss.at[0], a1, 0, flat)
    ar2 = reduce_copies(ss.at[1], a2, 15, tall)
    for copy in ar1:
        copy.start()
    for copy in g_halo:
        copy.start()

    lane = lax.broadcasted_iota(jnp.int32, (24, 128), 1)
    low_half = lax.broadcasted_iota(jnp.int32, (8, 128), 0) < 4

    def ring_row(block, n):
        beyond = jnp.where(low_half, block[n, 24:32], block[n, 0:8])
        return jnp.concatenate([block[n, 8:24], beyond], 0)

    def pack(block, which):
        def one(n, carry):
            high, low = carry
            row = ring_row(block, n)
            at = lane - HIGH * n
            high = jnp.where((at >= 0) & (at < HIGH), pltpu.roll(row, HIGH * n + 2, 1), high)
            at = lane - LOW * (n - 1)
            low = jnp.where((at >= 0) & (at < LOW), pltpu.roll(row, (LOW * n + 125) % 128, 1), low)
            return high, low

        zero = jnp.zeros((24, 128), jnp.float32)
        high, low = lax.fori_loop(0, rows + 2 * HALO, one, (zero, zero))
        packs[2 * which] = high
        packs[2 * which + 1] = low

    def pack_copies(which):
        peers = [(gx, gy, (gz + 3) % 4), (gx, gy, (gz + 1) % 4)]
        return [
            pltpu.make_async_remote_copy(
                src_ref=packs.at[2 * which + n],
                dst_ref=landed.at[2 * which + n],
                send_sem=h2_send.at[2 * which + n],
                recv_sem=h2_recv.at[2 * which + n],
                device_id=peer,
                device_id_type=MESH,
            )
            for n, peer in enumerate(peers)
        ]

    v_pack, g_pack = pack_copies(0), pack_copies(1)
    for copy in v_halo:
        copy.wait_recv()
    pack(xv, 0)
    for copy in v_pack:
        copy.start()

    for copy in ar1:
        copy.wait_recv()
    total = ss[0]
    for n in range(15):
        total = total + a1[n]
    ss[1] = total
    for copy in ar2:
        copy.start()

    for copy in g_halo:
        copy.wait_recv()
    pack(xg, 1)
    for copy in g_pack:
        copy.start()

    for copy in ar2:
        copy.wait_recv()
    total = ss[1]
    for n in range(15):
        total = total + a2[n]
    mean_square = jnp.sum(total, keepdims=True) * (1.0 / cells)
    scale = STEP_LENGTH * lax.rsqrt(mean_square + 1.0)

    def target_row(n, carry):
        t_out[n] = ring_row(xv, n) - scale * ring_row(xg, n)
        return carry

    lax.fori_loop(0, rows + 2 * HALO, target_row, 0)
    for copy in v_pack + g_pack:
        copy.wait_recv()
    eh_out[0] = packs[0] - scale * packs[2]
    el_out[0] = packs[1] - scale * packs[3]
    eh_out[1] = landed[0] - scale * landed[2]
    el_out[1] = landed[1] - scale * landed[3]

    for p in range(3):
        for hop in range(5):
            rs[p, hop].wait_send()
    for copy in v_halo + g_halo + v_pack + g_pack + ar1 + ar2:
        copy.wait_send()


def tv_kernel(sizes, t_in, eh_in, el_in, g_in, g_out, u_out, cur, bar, dx, dy, dz):
    nx, ny, nz = sizes
    gx, gy, gz = lax.axis_index("gx"), lax.axis_index("gy"), lax.axis_index("gz")
    rows = g_in.shape[0]
    lanes = 128
    shape = (24, 128)
    lane = lax.broadcasted_iota(jnp.int32, shape, 1)
    ring = lax.broadcasted_iota(jnp.int32, shape, 0)

    def steps(position, count):
        inside = (position >= 0) & (position < count - 1)
        return jnp.where(inside, jnp.float32(DUAL_STEP), jnp.float32(0.0))

    step_y = steps(gy * 16 + jnp.where(ring < 20, ring, ring - 24), ny)
    step_z = steps(gz * lanes + lane, nz)
    step_x = [steps(gx * rows + n - HALO, nx) for n in range(rows + 2 * HALO)]

    g_out[...] = g_in[...]

    def shrink(a, b, c):
        norm = a * a + b * b + c * c
        limit = TV_WEIGHT * TV_WEIGHT
        return jnp.where(norm > limit, TV_WEIGHT * lax.rsqrt(norm), 1.0)

    def up(field, axis, by=1):
        return pltpu.roll(field, field.shape[axis] - by, axis)

    def down(field, axis, by=1):
        return pltpu.roll(field, by, axis)

    def primal(current, spread, target_part):
        return (current + PRIMAL_STEP * spread + target_part) * (1.0 / (1.0 + PRIMAL_STEP))

    class Edge:
        def __init__(self, own, other, width, first_row, first_plane, mine):
            plane = lane % width
            self.width = width
            self.target = jnp.where(mine(plane), own, other)
            self.tpart = PRIMAL_STEP * self.target
            self.current = self.bar = self.target
            self.step_x = steps(gx * rows + first_row + lane // width, nx)
            self.step_z = steps(gz * lanes + first_plane + plane, nz)
            self.dual = None

        def ascend(self):
            b = self.bar
            a = self.step_x * (up(b, 1, self.width) - b)
            c = step_y * (up(b, 0) - b)
            d = self.step_z * (up(b, 1) - b)
            if self.dual is not None:
                a, c, d = self.dual[0] + a, self.dual[1] + c, self.dual[2] + d
            f = shrink(a, c, d)
            self.dual = (a * f, c * f, d * f)

        def descend(self):
            a, c, d = self.dual
            spread = (a - down(a, 1, self.width)) + (c - down(c, 0)) + (d - down(d, 1))
            new = primal(self.current, spread, self.tpart)
            self.bar = 2.0 * new - self.current
            self.current = new

    high = Edge(eh_in[0], eh_in[1], HIGH, -HALO, lanes - 2, lambda k: k < 2)
    low = Edge(el_in[0], el_in[1], LOW, 1 - HALO, -3, lambda k: k >= 3)

    last = lane == lanes - 1
    head = lane == 0
    for it in range(ITERS):
        final = it == ITERS - 1
        source = t_in if it == 0 else bar
        present = t_in if it == 0 else cur
        above = high.bar
        low.ascend()
        below = low.dual[2]
        if not final:
            low.descend()
            high.ascend()
            high.descend()
        stop = rows + 2 * HALO - 1 - it
        previous_dx = None
        here = source[it]
        for n in range(it, stop):
            after = source[n + 1]
            beyond = pltpu.roll(above, (lanes - 1 - (HIGH * n + 2)) % lanes, 1)
            a = step_x[n] * (after - here)
            b = step_y * (up(here, 0) - here)
            c = step_z * (jnp.where(last, beyond, up(here, 1)) - here)
            if it:
                a, b, c = dx[n] + a, dy[n] + b, dz[n] + c
            f = shrink(a, b, c)
            a, b, c = a * f, b * f, c * f
            if not final:
                dx[n], dy[n], dz[n] = a, b, c
            if n > it:
                under = pltpu.roll(below, (lanes - (LOW * (n - 1) + 2)) % lanes, 1)
                spread = (a - previous_dx) + (b - down(b, 0)) + (c - jnp.where(head, under, down(c, 1)))
                now = present[n]
                new = primal(now, spread, PRIMAL_STEP * t_in[n])
                if final:
                    u_out[n - HALO] = new[:16]
                else:
                    bar[n] = 2.0 * new - now
                    cur[n] = new
            previous_dx = a
            here = after


def shards(partials, code_bits, group_map, velocity):
    slots, nx, block_y, block_z = partials.shape
    block_x = velocity.shape[0]
    sizes = (
        block_x * lax.axis_size("gx"),
        block_y * lax.axis_size("gy"),
        block_z * lax.axis_size("gz"),
    )
    wide = block_x + 2 * HALO
    f32 = functools.partial(pltpu.VMEM, dtype=jnp.float32)
    dma = pltpu.SemaphoreType.DMA
    hbm = pl.BlockSpec(memory_space=pltpu.HBM)
    vmem = pl.BlockSpec(memory_space=pltpu.VMEM)
    packed = jax.ShapeDtypeStruct((2, 24, 128), jnp.float32)
    block = jax.ShapeDtypeStruct(velocity.shape, jnp.float32)
    target, high, low, gradient = pl.pallas_call(
        functools.partial(comm_kernel, sizes[0] * sizes[1] * sizes[2]),
        out_shape=(
            jax.ShapeDtypeStruct((wide, 24, 128), jnp.float32), packed, packed, block,
        ),
        in_specs=[hbm] * 4,
        out_specs=(vmem,) * 4,
        scratch_shapes=[
            f32(partials.shape),
            f32((8, block_x, 16, 128)),
            f32((7, block_x, 16, 128)),
            f32((wide, 32, 128)),
            f32((wide, 32, 128)),
            f32((4, 24, 128)),
            f32((4, 24, 128)),
            f32((2, 8, 128)),
            f32((15, 8, 128)),
            f32((15, 8, 128)),
            pltpu.SMEM(code_bits.shape, jnp.int32),
            pltpu.SMEM(group_map.shape, jnp.int32),
            dma((24,)), dma((3,)), dma((15,)), dma((15,)), dma((30,)), dma((30,)),
            dma((16,)), dma((16,)), dma((4,)), dma((4,)),
        ],
        compiler_params=pltpu.CompilerParams(
            collective_id=0, has_side_effects=True, vmem_limit_bytes=48 * 1024 * 1024
        ),
        name="decode_exchange",
    )(partials, code_bits, group_map, velocity)
    field = f32((wide, 24, 128))
    return pl.pallas_call(
        functools.partial(tv_kernel, sizes),
        out_shape=(block, block),
        in_specs=[vmem] * 4,
        out_specs=(vmem, vmem),
        scratch_shapes=[field] * 5,
        name="tv_steps",
    )(target, high, low, gradient)


def solution(mesh):
    split = P("gx", "gy", "gz")
    return jax.shard_map(
        shards,
        mesh=mesh,
        in_specs=(P("gx", None, "gy", "gz"), P(), P(), split),
        out_specs=(split, split),
        check_vma=False,
    )
```

time: 186 us -> 50.7 us (0.27); the launches traced: 184 us -> 50.5 us
  waiting for transfers between devices: 61.4 us -> 0 us
  starting transfers between devices: 59.2 us -> 0 us
  blocking collectives: 44.4 us -> 0 us
  Pallas kernels: 0 us -> 42.8 us
  matrix products: 4.61 us -> 0 us
  local copies, waits for them, and re-layouts: 10.1 us -> 6.98 us
  other arithmetic: 2.17 us -> 0 us
    ppermute x18 -> x0, starting transfers between devices: 52.8 us -> none  [from_behind(): return lax.ppermute(block, axis, route)]
    all_to_all x1 -> x0, waiting for transfers between devices: 47.9 us -> none  [shards(): lax.all_to_all(partials, GX, split_axis=1, concat_axis=0, tiled=True)]
    psum x5 -> x0, blocking collectives: 44.4 us -> none  [over_axes(): return functools.reduce(lax.psum, axes, shard)]
    pallas_call x0 -> x2, Pallas kernels: none -> 42.8 us  [the longest x1 37.1 us: shards(): pl.pallas_call(functools.partial(comm_kernel, sizes[0] * sizes[1] * sizes...]
    ppermute x18 -> x0, waiting for transfers between devices: 13.5 us -> none  [from_behind(): return lax.ppermute(block, axis, route)]
    all_to_all x1 -> x0, starting transfers between devices: 6.32 us -> none  [shards(): lax.all_to_all(partials, GX, split_axis=1, concat_axis=0, tiled=True)]
    dot_general x2 -> x0, matrix products: 4.61 us -> none  [the longest x1 4.35 us: shards(): jnp.einsum('gx,gxyz->xyz', local_signs, lax.all_to_all(partials, GX, spli...]
    all_to_all x1 -> x0, local copies, waits for them, and re-layouts: 2.76 us -> none  [shards(): lax.all_to_all(partials, GX, split_axis=1, concat_axis=0, tiled=True)]
  transfers between devices with their start and end apart: 19 -> 0, of which waited for: 7 -> 0; matrix products, arithmetic and copies ran while one was open for 0% -> 0% of each run, Pallas kernels for 0% -> 0%
where the time goes in v1:
time: 50.7 us; the launch traced here: 50.5 us
  Pallas kernels  42.8 us (84%)
  local copies, waits for them, and re-layouts  6.98 us (14%)
  between operations  0.66 us (1%)
    pallas_call x1, Pallas kernels, shards(): pl.pallas_call(functools.partial(comm_kernel, sizes[0] * sizes[1] * sizes...  37.1 us
    unnamed x16, local copies, waits for them, and re-layouts  6.98 us
    pallas_call x1, Pallas kernels, shards(): pl.pallas_call(functools.partial(tv_kernel, sizes), out_shape=(block, blo...  5.73 us

profile of v1, /device:TPU:1, one launch (start us, length us, event | category | flops | bytes accessed | tf_op | source)
XLA Modules:
  0.0 50.5 jit_solution(16752033360614556871)
XLA Ops:
  0.6 0.0 copy-start
  0.6 2.2 %copy-done = f32[4,128,16,128]{3,2,1,0:T(8,128)S(1)} copy-done((f32[4,128,16,128]{3,2,1,0:T(8,128)S(1)}, f32[4,128,16,128]{3,2,1,0:T(8,128)}, u32[]{:S(2)}) %copy-start) | copy-done | bytes 4194328
  2.8 0.0 copy-start.2
  2.8 0.9 %copy-done.2 = f32[16,16,128]{2,1,0:T(8,128)S(1)} copy-done((f32[16,16,128]{2,1,0:T(8,128)S(1)}, f32[16,16,128]{2,1,0:T(8,128)}, u32[]{:S(2)}) %copy-start.2) | copy-done | bytes 131096
  3.7 0.0 copy-start.6
  3.7 0.7 %copy-done.6 = s32[32,128]{1,0:T(8,128)S(1)} copy-done((s32[32,128]{1,0:T(8,128)S(1)}, s32[32,128]{1,0:T(8,128)}, u32[]{:S(2)}) %copy-start.6) | copy-done | bytes 16408
  4.4 0.0 copy-start.7
  4.4 0.7 %copy-done.7 = s32[32]{0:T(128)S(1)} copy-done((s32[32]{0:T(128)S(1)}, s32[32]{0:T(128)}, u32[]{:S(2)}) %copy-start.7) | copy-done | bytes 152
  5.1 37.1 %decode_exchange.1 = (f32[22,24,128]{2,1,0:T(8,128)S(1)}, f32[2,24,128]{2,1,0:T(8,128)S(1)}, f32[2,24,128]{2,1,0:T(8,128)S(1)}, f32[16,16,128]{2,1,0:T(8,128)S(1)}) custom-call(f32[4,128,16,128]{3,2,1,0:T(8,128)S(1)} %copy-done, s32[32,128]{1,0:T(8,128)S(1)} %copy-done.6, s32[32]{0:T(128)S(1)} %copy-done.7, f32[16,16,128]{2,1,0:T(8,128)S(1)} %copy-done.2), custom_call_target="tpu_custom_call" | custom-call | tf_op jit(solution)/shard_map/decode_exchange/pallas_call | solution.py:438
  42.2 0.0 copy-start.1
  42.2 0.7 %copy-done.1 = f32[22,24,128]{2,1,0:T(8,128)} copy-done((f32[22,24,128]{2,1,0:T(8,128)}, f32[22,24,128]{2,1,0:T(8,128)S(1)}, u32[]{:S(2)}) %copy-start.1) | copy-done | bytes 270360
  42.9 0.0 copy-start.3
  42.9 0.6 %copy-done.3 = f32[16,16,128]{2,1,0:T(8,128)} copy-done((f32[16,16,128]{2,1,0:T(8,128)}, f32[16,16,128]{2,1,0:T(8,128)S(1)}, u32[]{:S(2)}) %copy-start.3) | copy-done | bytes 131096
  43.5 0.0 copy-start.4
  43.5 0.6 %copy-done.4 = f32[2,24,128]{2,1,0:T(8,128)} copy-done((f32[2,24,128]{2,1,0:T(8,128)}, f32[2,24,128]{2,1,0:T(8,128)S(1)}, u32[]{:S(2)}) %copy-start.4) | copy-done | bytes 24600
  44.1 0.0 copy-start.5
  44.1 0.6 %copy-done.5 = f32[2,24,128]{2,1,0:T(8,128)} copy-done((f32[2,24,128]{2,1,0:T(8,128)}, f32[2,24,128]{2,1,0:T(8,128)S(1)}, u32[]{:S(2)}) %copy-start.5) | copy-done | bytes 24600
  44.7 5.7 %tv_steps.1 = (f32[16,16,128]{2,1,0:T(8,128)}, f32[16,16,128]{2,1,0:T(8,128)}) custom-call(f32[22,24,128]{2,1,0:T(8,128)} %copy-done.1, f32[2,24,128]{2,1,0:T(8,128)} %copy-done.4, f32[2,24,128]{2,1,0:T(8,128)} %copy-done.5, f32[16,16,128]{2,1,0:T(8,128)} %copy-done.3), custom_call_target="tpu_custom_call" | custom-call | tf_op jit(solution)/shard_map/tv_steps/pallas_call | solution.py:467
Async XLA Ops:
  0.6 2.2 %copy-start = (f32[4,128,16,128]{3,2,1,0:T(8,128)S(1)}, f32[4,128,16,128]{3,2,1,0:T(8,128)}, u32[]{:S(2)}) copy-start(f32[4,128,16,128]{3,2,1,0:T(8,128)} %partials.1) | copy-start | bytes 12582916
  2.8 0.9 %copy-start.2 = (f32[16,16,128]{2,1,0:T(8,128)S(1)}, f32[16,16,128]{2,1,0:T(8,128)}, u32[]{:S(2)}) copy-start(f32[16,16,128]{2,1,0:T(8,128)} %velocity.1) | copy-start | bytes 393220
  3.7 0.7 %copy-start.6 = (s32[32,128]{1,0:T(8,128)S(1)}, s32[32,128]{1,0:T(8,128)}, u32[]{:S(2)}) copy-start(s32[32,128]{1,0:T(8,128)} %code_bits.1) | copy-start | bytes 49156
  4.4 0.7 %copy-start.7 = (s32[32]{0:T(128)S(1)}, s32[32]{0:T(128)}, u32[]{:S(2)}) copy-start(s32[32]{0:T(128)} %group_map.1) | copy-start | bytes 388
  42.2 0.7 %copy-start.1 = (f32[22,24,128]{2,1,0:T(8,128)}, f32[22,24,128]{2,1,0:T(8,128)S(1)}, u32[]{:S(2)}) copy-start(f32[22,24,128]{2,1,0:T(8,128)S(1)} %get-tuple-element.6.t_in) | copy-start | bytes 811012
  42.9 0.6 %copy-start.3 = (f32[16,16,128]{2,1,0:T(8,128)}, f32[16,16,128]{2,1,0:T(8,128)S(1)}, u32[]{:S(2)}) copy-start(f32[16,16,128]{2,1,0:T(8,128)S(1)} %get-tuple-element.9.g_in) | copy-start | bytes 393220
  43.5 0.6 %copy-start.4 = (f32[2,24,128]{2,1,0:T(8,128)}, f32[2,24,128]{2,1,0:T(8,128)S(1)}, u32[]{:S(2)}) copy-start(f32[2,24,128]{2,1,0:T(8,128)S(1)} %get-tuple-element.7.eh_in) | copy-start | bytes 73732
  44.1 0.6 %copy-start.5 = (f32[2,24,128]{2,1,0:T(8,128)}, f32[2,24,128]{2,1,0:T(8,128)S(1)}, u32[]{:S(2)}) copy-start(f32[2,24,128]{2,1,0:T(8,128)S(1)} %get-tuple-element.8.el_in) | copy-start | bytes 73732

commit v2 on v1

--- a/solution.py
+++ b/solution.py
@@ -125,43 +125,53 @@
         rs[p, 3] = rs_copy(p, 3, slice(2, 3), slice(4, 5))
         rs[p, 4] = rs_copy(p, 4, slice(1, 2), slice(6, 7))
 
-    map_copy.wait()
-    bits_copy.wait()
-    for p in range(3):
-        weigh(7, p)
-        weigh(6, p)
-        if p == 0:
-            pl.semaphore_wait(barrier, len(greeted))
-        rs[p, 0].start()
-    for p in range(3):
-        weigh(5, p)
-        weigh(4, p)
-        rs[p, 1].start()
-    for p in range(3):
-        weigh(3, p)
-        weigh(2, p)
-    for p in range(3):
-        weigh(1, p)
-        weigh(0, p)
+    with jax.named_scope("load_bits"):
+        map_copy.wait()
+        bits_copy.wait()
+    with jax.named_scope("weigh_first"):
+        weigh(7, 0)
+        weigh(6, 0)
+    with jax.named_scope("entry_barrier"):
+        pl.semaphore_wait(barrier, len(greeted))
+    with jax.named_scope("weigh_sent"):
+        rs[0, 0].start()
+        for p in (1, 2):
+            weigh(7, p)
+            weigh(6, p)
+            rs[p, 0].start()
+        for p in range(3):
+            weigh(5, p)
+            weigh(4, p)
+            rs[p, 1].start()
+    with jax.named_scope("weigh_rest"):
+        for p in range(3):
+            weigh(3, p)
+            weigh(2, p)
+        for p in range(3):
+            weigh(1, p)
+            weigh(0, p)
 
     def gather_in(p, k, source):
         r0, r1 = STREAMS[p]
         w[k, r0:r1] = w[k, r0:r1] + r[source, r0:r1]
 
     for p in range(3):
-        rs[p, 0].wait_recv()
-        gather_in(p, 3, 3)
-        rs[p, 2].start()
-        gather_in(p, 2, 2)
-        rs[p, 3].start()
+        with jax.named_scope(f"hop1a#p={p}"):
+            rs[p, 0].wait_recv()
+            gather_in(p, 3, 3)
+            rs[p, 2].start()
+            gather_in(p, 2, 2)
+            rs[p, 3].start()
     for p in range(3):
-        rs[p, 1].wait_recv()
-        gather_in(p, 1, 1)
-        gather_in(p, 0, 0)
+        with jax.named_scope(f"hop1b#p={p}"):
+            rs[p, 1].wait_recv()
+            gather_in(p, 1, 1)
+            gather_in(p, 0, 0)
     for p in range(3):
-        rs[p, 2].wait_recv()
-        gather_in(p, 1, 5)
-        rs[p, 4].start()
+        with jax.named_scope(f"hop2a#p={p}"):
+            rs[p, 2].wait_recv()
+            gather_in(p, 1, 5)
+            rs[p, 4].start()
 
     def halo_copies(block, which):
         down, up = slice(HALO, 2 * HALO), slice(rows, rows + HALO)
@@ -191,23 +201,26 @@
 
     v_halo = halo_copies(xv, 0)
     g_halo = halo_copies(xg, 1)
-    vel_copy.wait()
-    for copy in v_halo:
-        copy.start()
-
+    with jax.named_scope("velocity_halo"):
+        vel_copy.wait()
+        for copy in v_halo:
+            copy.start()
+
+    with jax.named_scope("hop2b"):
+        for p in range(3):
+            rs[p, 3].wait_recv()
+            gather_in(p, 0, 4)
     square = jnp.zeros((8, 128), jnp.float32)
-    for p, (r0, r1) in enumerate(STREAMS):
-        rs[p, 3].wait_recv()
-        gather_in(p, 0, 4)
-    for p, (r0, r1) in enumerate(STREAMS):
-        rs[p, 4].wait_recv()
-        for n in range(r0, r1):
-            value = w[0, n] + r[6, n]
-            xg[HALO + n, 8:24] = value
-            g_out[n] = value
-            value = value * value
-            square = square + (value[:8] + value[8:])
-    ss[0] = square
+    with jax.named_scope("hop3"):
+        for p, (r0, r1) in enumerate(STREAMS):
+            rs[p, 4].wait_recv()
+            for n in range(r0, r1):
+                value = w[0, n] + r[6, n]
+                xg[HALO + n, 8:24] = value
+                g_out[n] = value
+                value = value * value
+                square = square + (value[:8] + value[8:])
+        ss[0] = square
 
     def reduce_copies(src, dst, base, peers):
         return [
@@ -224,10 +237,11 @@
 
     ar1 = reduce_copies(ss.at[0], a1, 0, flat)
     ar2 = reduce_copies(ss.at[1], a2, 15, tall)
-    for copy in ar1:
-        copy.start()
-    for copy in g_halo:
-        copy.start()
+    with jax.named_scope("send_squares"):
+        for copy in ar1:
+            copy.start()
+        for copy in g_halo:
+            copy.start()
 
     lane = lax.broadcasted_iota(jnp.int32, (24, 128), 1)
     low_half = lax.broadcasted_iota(jnp.int32, (8, 128), 0) < 4
@@ -266,29 +280,35 @@
         ]
 
     v_pack, g_pack = pack_copies(0), pack_copies(1)
-    for copy in v_halo:
-        copy.wait_recv()
-    pack(xv, 0)
-    for copy in v_pack:
-        copy.start()
-
-    for copy in ar1:
-        copy.wait_recv()
-    total = ss[0]
-    for n in range(15):
-        total = total + a1[n]
-    ss[1] = total
-    for copy in ar2:
-        copy.start()
-
-    for copy in g_halo:
-        copy.wait_recv()
-    pack(xg, 1)
-    for copy in g_pack:
-        copy.start()
-
-    for copy in ar2:
-        copy.wait_recv()
+    with jax.named_scope("wait_v_halo"):
+        for copy in v_halo:
+            copy.wait_recv()
+    with jax.named_scope("pack_v"):
+        pack(xv, 0)
+        for copy in v_pack:
+            copy.start()
+
+    with jax.named_scope("wait_squares1"):
+        for copy in ar1:
+            copy.wait_recv()
+        total = ss[0]
+        for n in range(15):
+            total = total + a1[n]
+        ss[1] = total
+        for copy in ar2:
+            copy.start()
+
+    with jax.named_scope("wait_g_halo"):
+        for copy in g_halo:
+            copy.wait_recv()
+    with jax.named_scope("pack_g"):
+        pack(xg, 1)
+        for copy in g_pack:
+            copy.start()
+
+    with jax.named_scope("wait_squares2"):
+        for copy in ar2:
+            copy.wait_recv()
     total = ss[1]
     for n in range(15):
         total = total + a2[n]
@@ -299,22 +319,25 @@
         t_out[n] = ring_row(xv, n) - scale * ring_row(xg, n)
         return carry
 
-    lax.fori_loop(0, rows + 2 * HALO, target_row, 0)
-    for copy in v_pack + g_pack:
-        copy.wait_recv()
-    eh_out[0] = packs[0] - scale * packs[2]
-    el_out[0] = packs[1] - scale * packs[3]
-    eh_out[1] = landed[0] - scale * landed[2]
-    el_out[1] = landed[1] - scale * landed[3]
-
-    for p in range(3):
-        for hop in range(5):
-            rs[p, hop].wait_send()
-    for copy in v_halo + g_halo + v_pack + g_pack + ar1 + ar2:
-        copy.wait_send()
-
-
-def tv_kernel(sizes, t_in, eh_in, el_in, g_in, g_out, u_out, cur, bar, dx, dy, dz):
+    with jax.named_scope("target"):
+        lax.fori_loop(0, rows + 2 * HALO, target_row, 0)
+    with jax.named_scope("wait_packs"):
+        for copy in v_pack + g_pack:
+            copy.wait_recv()
+        eh_out[0] = packs[0] - scale * packs[2]
+        el_out[0] = packs[1] - scale * packs[3]
+        eh_out[1] = landed[0] - scale * landed[2]
+        el_out[1] = landed[1] - scale * landed[3]
+
+    with jax.named_scope("drain"):
+        for p in range(3):
+            for hop in range(5):
+                rs[p, hop].wait_send()
+        for copy in v_halo + g_halo + v_pack + g_pack + ar1 + ar2:
+            copy.wait_send()
+
+
+def tv_kernel(sizes, t_in, eh_in, el_in, g_in, g_out, u_hbm, cur, bar, dx, dy, dz, u_out, out_sem):
     nx, ny, nz = sizes
     gx, gy, gz = lax.axis_index("gx"), lax.axis_index("gy"), lax.axis_index("gz")
     rows = g_in.shape[0]
@@ -331,7 +354,8 @@
     step_z = steps(gz * lanes + lane, nz)
     step_x = [steps(gx * rows + n - HALO, nx) for n in range(rows + 2 * HALO)]
 
-    g_out[...] = g_in[...]
+    g_copy = pltpu.make_async_copy(g_in, g_out, out_sem.at[0])
+    g_copy.start()
 
     def shrink(a, b, c):
         norm = a * a + b * b + c * c
@@ -419,6 +443,11 @@
             previous_dx = a
             here = after
 
+    u_copy = pltpu.make_async_copy(u_out, u_hbm, out_sem.at[1])
+    u_copy.start()
+    g_copy.wait()
+    u_copy.wait()
+
 
 def shards(partials, code_bits, group_map, velocity):
     slots, nx, block_y, block_z = partials.shape
@@ -433,12 +462,13 @@
     dma = pltpu.SemaphoreType.DMA
     hbm = pl.BlockSpec(memory_space=pltpu.HBM)
     vmem = pl.BlockSpec(memory_space=pltpu.VMEM)
-    packed = jax.ShapeDtypeStruct((2, 24, 128), jnp.float32)
-    block = jax.ShapeDtypeStruct(velocity.shape, jnp.float32)
+    packed = f32((2, 24, 128))
+    block = f32(velocity.shape)
+    result = pltpu.HBM(velocity.shape, jnp.float32)
     target, high, low, gradient = pl.pallas_call(
         functools.partial(comm_kernel, sizes[0] * sizes[1] * sizes[2]),
         out_shape=(
-            jax.ShapeDtypeStruct((wide, 24, 128), jnp.float32), packed, packed, block,
+            f32((wide, 24, 128)), packed, packed, block,
         ),
         in_specs=[hbm] * 4,
         out_specs=(vmem,) * 4,
@@ -462,16 +492,17 @@
             collective_id=0, has_side_effects=True, vmem_limit_bytes=48 * 1024 * 1024
         ),
         name="decode_exchange",
-    )(partials, code_bits, group_map, velocity)
+    )(*(pltpu.with_memory_space_constraint(a, pltpu.HBM) for a in (partials, code_bits, group_map, velocity)))
     field = f32((wide, 24, 128))
     return pl.pallas_call(
         functools.partial(tv_kernel, sizes),
-        out_shape=(block, block),
+        out_shape=(result, result),
         in_specs=[vmem] * 4,
-        out_specs=(vmem, vmem),
-        scratch_shapes=[field] * 5,
+        out_specs=(hbm, hbm),
+        scratch_shapes=[field] * 5 + [block, dma((2,))],
+        compiler_params=pltpu.CompilerParams(vmem_limit_bytes=32 * 1024 * 1024),
         name="tv_steps",
-    )(target, high, low, gradient)
+    )(*(pltpu.with_memory_space_constraint(a, pltpu.VMEM) for a in (target, high, low, gradient)))
 
 
 def solution(mesh):

time: 50.7 us -> 41.4 us (0.82)
  local copies, waits for them, and re-layouts: 6.98 us -> 0 us
  Pallas kernels: 42.8 us -> 40.7 us
    unnamed x16 -> x0, local copies, waits for them, and re-layouts: 6.98 us -> none
    pallas_call x1, Pallas kernels: 37.1 us -> 35.9 us  [shards(): pl.pallas_call(functools.partial(comm_kernel, sizes[0] * sizes[1] * sizes...]
    pallas_call x1, Pallas kernels: 5.73 us -> 4.73 us  [shards(): pl.pallas_call(functools.partial(tv_kernel, sizes), out_shape=(result, re...]
where the time goes in v2:
time: 41.4 us; the launch traced here: 41.3 us
  Pallas kernels  40.7 us (98%)
  between operations  0.64 us (2%)
    pallas_call x1, Pallas kernels, shards(): pl.pallas_call(functools.partial(comm_kernel, sizes[0] * sizes[1] * sizes...  35.9 us
    pallas_call x1, Pallas kernels, shards(): pl.pallas_call(functools.partial(tv_kernel, sizes), out_shape=(result, re...  4.73 us

profile of v2, /device:TPU:1, one launch (start us, length us, event | category | flops | bytes accessed | tf_op | source)
XLA Modules:
  0.0 41.3 jit_solution(1844570127186762469)
XLA Ops:
  0.6 35.9 %decode_exchange.1 = (f32[22,24,128]{2,1,0:T(8,128)S(1)}, f32[2,24,128]{2,1,0:T(8,128)S(1)}, f32[2,24,128]{2,1,0:T(8,128)S(1)}, f32[16,16,128]{2,1,0:T(8,128)S(1)}) custom-call(f32[4,128,16,128]{3,2,1,0:T(8,128)} %partials.1, s32[32,128]{1,0:T(8,128)} %code_bits.1, s32[32]{0:T(128)} %group_map.1, f32[16,16,128]{2,1,0:T(8,128)} %velocity.1), custom_call_target="tpu_custom_call" | custom-call | tf_op jit(solution)/shard_map/decode_exchange/pallas_call | solution.py:468
  36.6 4.7 %tv_steps.1 = (f32[16,16,128]{2,1,0:T(8,128)}, f32[16,16,128]{2,1,0:T(8,128)}) custom-call(f32[22,24,128]{2,1,0:T(8,128)S(1)} %get-tuple-element.6.t_in, f32[2,24,128]{2,1,0:T(8,128)S(1)} %get-tuple-element.7.eh_in, f32[2,24,128]{2,1,0:T(8,128)S(1)} %get-tuple-element.8.el_in, f32[16,16,128]{2,1,0:T(8,128)S(1)} %get-tuple-element.9.g_in), custom_call_target="tpu_custom_call" | custom-call | tf_op jit(solution)/shard_map/tv_steps/pallas_call | solution.py:497

commit v3 on v2

v3 whole, which is shorter than its diff:
```python
import functools

import jax
import jax.numpy as jnp
from jax import lax
from jax.experimental import pallas as pl
from jax.experimental.pallas import tpu as pltpu
from jax.sharding import PartitionSpec as P

ITERS = 3
HALO = 3
STEP_LENGTH = 0.5
TV_WEIGHT = 0.2
DUAL_STEP = 0.28
PRIMAL_STEP = 0.28
MESH = pl.DeviceIdType.MESH

STREAMS = ((0, 5), (5, 10), (10, 16))
ORDERS = ((0, 1, 2), (1, 2, 0), (2, 0, 1))
HIGH = 5
LOW = 6


def flipped(x, zl, bits):
    bz, bp, bq = bits
    if bz:
        zl = 1 - zl
    if bp:
        x = x + 1 - 2 * (x % 2)
    if bq:
        x = 3 - x
    return x * 2 + zl


def cube_bits(order, idx):
    bits = [0, 0, 0]
    for place, dim in enumerate(order):
        bits[dim] = (idx >> (2 - place)) & 1
    return tuple(bits)


def comm_kernel(
    cells,
    partials, code_bits, group_map, velocity,
    t_out, eh_out, el_out, g_out,
    pin, w, r, vel, faces, sides, ends, packs, landed, ring_g, ss, a1, a2, bits_s, map_s,
    load_sem, small_sem, rs_send, rs_recv, ar_sem, halo_sem, pack_sem, met,
):
    gx, gy, gz = lax.axis_index("gx"), lax.axis_index("gy"), lax.axis_index("gz")
    x, zl = gx // 2, gx % 2
    zh, core = gy // 2, gy % 2
    z = zh * 2 + zl
    slots = partials.shape[0]
    rows = w.shape[1]
    wide = rows + 2 * HALO

    def along_x(step):
        return (((x + step + 4) % 4) * 2 + zl, gy, gz)

    def along_y(step):
        return (gx, gy, (gz + step + 4) % 4)

    def along_z(step):
        zz = (z + step + 8) % 8
        return (x * 2 + zz % 2, (zz // 2) * 2 + core, gz)

    def remote(src, dst, send_sem, recv_sem, peer):
        return pltpu.make_async_remote_copy(
            src_ref=src, dst_ref=dst, send_sem=send_sem, recv_sem=recv_sem,
            device_id=peer, device_id_type=MESH,
        )

    bits_copy = pltpu.make_async_copy(code_bits, bits_s, small_sem.at[0])
    map_copy = pltpu.make_async_copy(group_map, map_s, small_sem.at[1])
    vel_copy = pltpu.make_async_copy(velocity, vel, small_sem.at[2])
    map_copy.start()
    bits_copy.start()

    near = [along_x(1), along_x(-1), along_y(1), along_y(-1), along_z(1), along_z(-1)]
    near.append((gx, zh * 2 + 1 - core, gz))
    barrier = pltpu.get_barrier_semaphore()
    for peer in near:
        pl.semaphore_signal(barrier, inc=1, device_id=peer, device_id_type=MESH)

    def load_span(idx, p):
        r0, r1 = STREAMS[p]
        dest = flipped(x, zl, cube_bits(ORDERS[p], idx))
        return dest * rows + r0, r1 - r0

    for pair in (3, 2, 1, 0):
        for idx in (2 * pair + 1, 2 * pair):
            for p in range(3):
                start, count = load_span(idx, p)
                span = pl.ds(start, count)
                pltpu.make_async_copy(
                    partials.at[:, span], pin.at[:, span], load_sem.at[p * 4 + pair]
                ).start()
    vel_copy.start()

    def weigh(idx, p):
        start, count = load_span(idx, p)
        if idx % 2:
            both = pl.ds(0, 2 * count)
            pltpu.make_async_copy(
                partials.at[:, both], pin.at[:, both], load_sem.at[p * 4 + idx // 2]
            ).wait()
        for n in range(count):
            total = None
            for i in range(slots):
                sign = 2.0 * bits_s[map_s[gx * slots + i], start + n].astype(jnp.float32) - 1.0
                term = sign * pin[i, start + n]
                total = term if total is None else total + term
            w[idx, STREAMS[p][0] + n] = total

    sends = ((7, 3, 0), (6, 2, 0), (5, 1, 0), (4, 0, 0), (3, 5, 1), (2, 4, 1), (1, 6, 2))
    rs = {}
    for p, (r0, r1) in enumerate(STREAMS):
        for n, (src, dst, place) in enumerate(sends):
            step = [0, 0, 0]
            step[ORDERS[p][place]] = 1
            rs[p, src] = remote(
                w.at[src, r0:r1], r.at[dst, r0:r1], rs_send.at[0], rs_recv.at[p * 7 + n],
                (flipped(x, zl, step), gy, gz),
            )

    def meet(which, peers):
        for peer in peers:
            pl.semaphore_signal(met.at[which], inc=1, device_id=peer, device_id_type=MESH)

    with jax.named_scope("load_bits"):
        map_copy.wait()
        bits_copy.wait()
    with jax.named_scope("weigh_first"):
        weigh(7, 0)
    with jax.named_scope("entry_barrier"):
        pl.semaphore_wait(barrier, len(near))
    with jax.named_scope("weigh_sent"):
        rs[0, 7].start()
        for p in (1, 2):
            weigh(7, p)
            rs[p, 7].start()
        for idx in (6, 5):
            for p in range(3):
                weigh(idx, p)
                rs[p, idx].start()
    with jax.named_scope("weigh_rest"):
        meet(0, [along_y(1), along_y(-1), along_z(1), along_z(-1)])
        for idx in (3, 4, 2, 1, 0):
            for p in range(3):
                weigh(idx, p)

    low_half = lax.broadcasted_iota(jnp.int32, (8, 128), 0) < 4

    def fold_faces(block, which):
        for k in range(8):
            faces[which, 0, k] = jnp.where(low_half, pltpu.roll(block[k + 8, 8:16], 4, 0), block[k, 8:16])
            faces[which, 1, k] = jnp.where(low_half, block[k, 0:8], pltpu.roll(block[k + 8, 0:8], 4, 0))

    with jax.named_scope("meet_more"):
        vel_copy.wait()
        fold_faces(vel, 0)
        pl.semaphore_wait(met.at[0], 4)
        meet(1, [along_x(1), along_x(-1), along_z(2), along_z(-2)])

    def add_in(p, k, *sources):
        r0, r1 = STREAMS[p]
        for n in range(r0, r1):
            total = w[k, n]
            for source in sources:
                total = total + r[source, n]
            w[k, n] = total

    for p in range(3):
        with jax.named_scope(f"hop1a#p={p}"):
            rs[p, 7].wait_recv()
            add_in(p, 3, 3)
            rs[p, 3].start()
            rs[(p + 1) % 3, 4].start()
    for p in range(3):
        with jax.named_scope(f"hop1b#p={p}"):
            rs[p, 6].wait_recv()
            add_in(p, 2, 2)
            rs[p, 2].start()
    with jax.named_scope("meet_last"):
        pl.semaphore_wait(met.at[1], 4)
        meet(2, [along_x(1), along_x(-1)])
    for p in range(3):
        with jax.named_scope(f"hop2a#p={p}"):
            rs[p, 5].wait_recv()
            rs[p, 3].wait_recv()
            add_in(p, 1, 1, 5)
            rs[p, 1].start()

    gx_up, gx_down = (gx + 1) % 8, (gx + 7) % 8
    gy_up, gy_down = (gy + 1) % 8, (gy + 7) % 8

    def halo_copies(block, which):
        side = [
            ((gx, gy_up, gz), 0, slice(0, 8), slice(3, 11)),
            ((gx, gy_down, gz), 1, slice(0, 8), slice(3, 11)),
            ((gx_up, gy_up, gz), 0, slice(5, 8), slice(0, 3)),
            ((gx_up, gy_down, gz), 1, slice(5, 8), slice(0, 3)),
            ((gx_down, gy_up, gz), 0, slice(0, 3), slice(11, 14)),
            ((gx_down, gy_down, gz), 1, slice(0, 3), slice(11, 14)),
        ]
        end = [
            ((gx_up, gy, gz), slice(rows - HALO, rows), slice(0, 3)),
            ((gx_down, gy, gz), slice(0, HALO), slice(3, 6)),
        ]
        sem = [halo_sem.at[which * 3 + k] for k in range(3)]
        return [
            remote(faces.at[which, d, src], sides.at[which, d, dst], sem[0], sem[1], peer)
            for peer, d, src, dst in side
        ] + [
            remote(block.at[src], ends.at[which, dst], sem[0], sem[2], peer)
            for peer, src, dst in end
        ]

    def halo_waits(which):
        sem = [halo_sem.at[which * 3 + k] for k in range(3)]
        return (
            remote(sides.at[which], sides.at[which], sem[0], sem[1], along_y(1)),
            remote(ends.at[which], ends.at[which], sem[0], sem[2], along_y(1)),
        )

    with jax.named_scope("velocity_halo"):
        pl.semaphore_wait(met.at[2], 2)
        for copy in halo_copies(vel, 0):
            copy.start()

    for p in range(3):
        with jax.named_scope(f"hop2b#p={p}"):
            rs[p, 4].wait_recv()
            rs[p, 2].wait_recv()
            add_in(p, 0, 0, 4)
    square = jnp.zeros((8, 128), jnp.float32)
    for p, (r0, r1) in enumerate(STREAMS):
        with jax.named_scope(f"hop3#p={p}"):
            rs[p, 1].wait_recv()
            for n in range(r0, r1):
                value = w[0, n] + r[6, n]
                g_out[n] = value
                value = value * value
                square = square + (value[:8] + value[8:])
    ss[0] = square

    flat = [
        (((x + rx) % 4) * 2 + zl, gy, (gz + ry) % 4)
        for rx in range(4) for ry in range(4) if rx or ry
    ]
    tall = []
    for rz in range(8):
        for rc in range(2):
            if rz or rc:
                zz = (z + rz) % 8
                tall.append((x * 2 + zz % 2, (zz // 2) * 2 + (core + rc) % 2, gz))

    with jax.named_scope("send_squares"):
        for n, peer in enumerate(flat):
            remote(ss.at[0], a1.at[n], ar_sem.at[0], ar_sem.at[1], peer).start()
        fold_faces(g_out, 1)
        for copy in halo_copies(g_out, 1):
            copy.start()

    lane = lax.broadcasted_iota(jnp.int32, (24, 128), 1)

    def ring_row(block, which, n):
        inner = ends[which, n] if n < HALO else block[n - HALO] if n < rows + HALO else ends[which, n - rows]
        k = n if n < 11 else n - 8
        below, above = sides[which, 0, k], sides[which, 1, k]
        if n < HALO or 11 <= n < rows + HALO:
            beyond = pltpu.roll(jnp.where(low_half, below, above), 4, 0)
        else:
            beyond = jnp.where(low_half, above, below)
        return jnp.concatenate([inner, beyond], 0)

    def pack(block, which, ring):
        high = low = jnp.zeros((24, 128), jnp.float32)
        for n in range(wide):
            row = ring_row(block, which, n)
            ring[n] = row
            mine = (lane >= HIGH * n) & (lane < HIGH * (n + 1))
            high = jnp.where(mine, pltpu.roll(row, HIGH * n + 2, 1), high)
            if n:
                mine = (lane >= LOW * (n - 1)) & (lane < LOW * n)
                low = jnp.where(mine, pltpu.roll(row, (LOW * n + 125) % 128, 1), low)
        packs[2 * which] = high
        packs[2 * which + 1] = low
        for n, step in ((0, -1), (1, 1)):
            k = 2 * which + n
            remote(
                packs.at[k], landed.at[k], pack_sem.at[2 * which], pack_sem.at[2 * which + 1], along_y(step)
            ).start()

    def pack_wait(which):
        both = slice(2 * which, 2 * which + 2)
        return remote(
            packs.at[both], landed.at[both], pack_sem.at[2 * which], pack_sem.at[2 * which + 1], along_y(1)
        )

    squares1 = remote(a1, a1, ar_sem.at[0], ar_sem.at[1], along_y(1))
    squares2 = remote(a2, a2, ar_sem.at[2], ar_sem.at[3], along_y(1))
    with jax.named_scope("wait_squares1"):
        squares1.wait_recv()
        total = ss[0]
        for n in range(15):
            total = total + a1[n]
        ss[1] = total
        for n, peer in enumerate(tall):
            remote(ss.at[1], a2.at[n], ar_sem.at[2], ar_sem.at[3], peer).start()

    with jax.named_scope("wait_v_halo"):
        for copy in halo_waits(0):
            copy.wait_recv()
    with jax.named_scope("pack_v"):
        pack(vel, 0, t_out)
    with jax.named_scope("wait_g_halo"):
        for copy in halo_waits(1):
            copy.wait_recv()
    with jax.named_scope("pack_g"):
        pack(g_out, 1, ring_g)
    with jax.named_scope("wait_packs"):
        pack_wait(0).wait_recv()
        pack_wait(1).wait_recv()

    with jax.named_scope("wait_squares2"):
        squares2.wait_recv()
    with jax.named_scope("target"):
        total = ss[1]
        for n in range(15):
            total = total + a2[n]
        mean_square = jnp.sum(total, keepdims=True) * (1.0 / cells)
        scale = STEP_LENGTH * lax.rsqrt(mean_square + 1.0)
        for n in range(wide):
            t_out[n] = t_out[n] - scale * ring_g[n]
        for n, out in ((0, eh_out), (1, el_out)):
            out[0] = packs[n] - scale * packs[2 + n]
            out[1] = landed[n] - scale * landed[2 + n]

    with jax.named_scope("drain"):
        remote(r, r, rs_send.at[0], rs_recv.at[0], along_y(1)).wait_send()
        squares1.wait_send()
        squares2.wait_send()
        for which in range(2):
            for copy in halo_waits(which):
                copy.wait_send()
            pack_wait(which).wait_send()


def tv_kernel(sizes, t_in, eh_in, el_in, g_in, g_out, u_hbm, cur, bar, dx, dy, dz, u_out, out_sem):
    nx, ny, nz = sizes
    gx, gy, gz = lax.axis_index("gx"), lax.axis_index("gy"), lax.axis_index("gz")
    rows = g_in.shape[0]
    lanes = 128
    shape = (24, 128)
    lane = lax.broadcasted_iota(jnp.int32, shape, 1)
    ring = lax.broadcasted_iota(jnp.int32, shape, 0)

    def steps(position, count):
        inside = (position >= 0) & (position < count - 1)
        return jnp.where(inside, jnp.float32(DUAL_STEP), jnp.float32(0.0))

    step_y = steps(gy * 16 + jnp.where(ring < 20, ring, ring - 24), ny)
    step_z = steps(gz * lanes + lane, nz)
    step_x = [steps(gx * rows + n - HALO, nx) for n in range(rows + 2 * HALO)]

    g_copy = pltpu.make_async_copy(g_in, g_out, out_sem.at[0])
    g_copy.start()

    def shrink(a, b, c):
        norm = a * a + b * b + c * c
        limit = TV_WEIGHT * TV_WEIGHT
        return jnp.where(norm > limit, TV_WEIGHT * lax.rsqrt(norm), 1.0)

    def up(field, axis, by=1):
        return pltpu.roll(field, field.shape[axis] - by, axis)

    def down(field, axis, by=1):
        return pltpu.roll(field, by, axis)

    def primal(current, spread, target_part):
        return (current + PRIMAL_STEP * spread + target_part) * (1.0 / (1.0 + PRIMAL_STEP))

    class Edge:
        def __init__(self, own, other, width, first_row, first_plane, mine):
            plane = lane % width
            self.width = width
            self.target = jnp.where(mine(plane), own, other)
            self.tpart = PRIMAL_STEP * self.target
            self.current = self.bar = self.target
            self.step_x = steps(gx * rows + first_row + lane // width, nx)
            self.step_z = steps(gz * lanes + first_plane + plane, nz)
            self.dual = None

        def ascend(self):
            b = self.bar
            a = self.step_x * (up(b, 1, self.width) - b)
            c = step_y * (up(b, 0) - b)
            d = self.step_z * (up(b, 1) - b)
            if self.dual is not None:
                a, c, d = self.dual[0] + a, self.dual[1] + c, self.dual[2] + d
            f = shrink(a, c, d)
            self.dual = (a * f, c * f, d * f)

        def descend(self):
            a, c, d = self.dual
            spread = (a - down(a, 1, self.width)) + (c - down(c, 0)) + (d - down(d, 1))
            new = primal(self.current, spread, self.tpart)
            self.bar = 2.0 * new - self.current
            self.current = new

    high = Edge(eh_in[0], eh_in[1], HIGH, -HALO, lanes - 2, lambda k: k < 2)
    low = Edge(el_in[0], el_in[1], LOW, 1 - HALO, -3, lambda k: k >= 3)

    last = lane == lanes - 1
    head = lane == 0
    for it in range(ITERS):
        final = it == ITERS - 1
        source = t_in if it == 0 else bar
        present = t_in if it == 0 else cur
        above = high.bar
        low.ascend()
        below = low.dual[2]
        if not final:
            low.descend()
            high.ascend()
            high.descend()
        stop = rows + 2 * HALO - 1 - it
        previous_dx = None
        here = source[it]
        for n in range(it, stop):
            after = source[n + 1]
            beyond = pltpu.roll(above, (lanes - 1 - (HIGH * n + 2)) % lanes, 1)
            a = step_x[n] * (after - here)
            b = step_y * (up(here, 0) - here)
            c = step_z * (jnp.where(last, beyond, up(here, 1)) - here)
            if it:
                a, b, c = dx[n] + a, dy[n] + b, dz[n] + c
            f = shrink(a, b, c)
            a, b, c = a * f, b * f, c * f
            if not final:
                dx[n], dy[n], dz[n] = a, b, c
            if n > it:
                under = pltpu.roll(below, (lanes - (LOW * (n - 1) + 2)) % lanes, 1)
                spread = (a - previous_dx) + (b - down(b, 0)) + (c - jnp.where(head, under, down(c, 1)))
                now = present[n]
                new = primal(now, spread, PRIMAL_STEP * t_in[n])
                if final:
                    u_out[n - HALO] = new[:16]
                else:
                    bar[n] = 2.0 * new - now
                    cur[n] = new
            previous_dx = a
            here = after

    u_copy = pltpu.make_async_copy(u_out, u_hbm, out_sem.at[1])
    u_copy.start()
    g_copy.wait()
    u_copy.wait()


def shards(partials, code_bits, group_map, velocity):
    slots, nx, block_y, block_z = partials.shape
    block_x = velocity.shape[0]
    sizes = (
        block_x * lax.axis_size("gx"),
        block_y * lax.axis_size("gy"),
        block_z * lax.axis_size("gz"),
    )
    wide = block_x + 2 * HALO
    f32 = functools.partial(pltpu.VMEM, dtype=jnp.float32)
    dma = pltpu.SemaphoreType.DMA
    hbm = pl.BlockSpec(memory_space=pltpu.HBM)
    vmem = pl.BlockSpec(memory_space=pltpu.VMEM)
    packed = f32((2, 24, 128))
    block = f32(velocity.shape)
    result = pltpu.HBM(velocity.shape, jnp.float32)
    target, high, low, gradient = pl.pallas_call(
        functools.partial(comm_kernel, sizes[0] * sizes[1] * sizes[2]),
        out_shape=(
            f32((wide, 24, 128)), packed, packed, block,
        ),
        in_specs=[hbm] * 4,
        out_specs=(vmem,) * 4,
        scratch_shapes=[
            f32(partials.shape),
            f32((8, block_x, 16, 128)),
            f32((7, block_x, 16, 128)),
            block,
            f32((2, 2, 8, 8, 128)),
            f32((2, 2, 14, 8, 128)),
            f32((2, 6, 16, 128)),
            f32((4, 24, 128)),
            f32((4, 24, 128)),
            f32((wide, 24, 128)),
            f32((2, 8, 128)),
            f32((15, 8, 128)),
            f32((15, 8, 128)),
            pltpu.SMEM(code_bits.shape, jnp.int32),
            pltpu.SMEM(group_map.shape, jnp.int32),
            dma((12,)), dma((3,)), dma((1,)), dma((21,)), dma((4,)), dma((6,)), dma((4,)),
            pltpu.SemaphoreType.REGULAR((3,)),
        ],
        compiler_params=pltpu.CompilerParams(
            collective_id=0, has_side_effects=True, vmem_limit_bytes=48 * 1024 * 1024
        ),
        name="decode_exchange",
    )(*(pltpu.with_memory_space_constraint(a, pltpu.HBM) for a in (partials, code_bits, group_map, velocity)))
    field = f32((wide, 24, 128))
    return pl.pallas_call(
        functools.partial(tv_kernel, sizes),
        out_shape=(result, result),
        in_specs=[vmem] * 4,
        out_specs=(hbm, hbm),
        scratch_shapes=[field] * 5 + [block, dma((2,))],
        compiler_params=pltpu.CompilerParams(vmem_limit_bytes=32 * 1024 * 1024),
        name="tv_steps",
    )(*(pltpu.with_memory_space_constraint(a, pltpu.VMEM) for a in (target, high, low, gradient)))


def solution(mesh):
    split = P("gx", "gy", "gz")
    return jax.shard_map(
        shards,
        mesh=mesh,
        in_specs=(P("gx", None, "gy", "gz"), P(), P(), split),
        out_specs=(split, split),
        check_vma=False,
    )
```

time: 41.4 us -> 36.4 us (0.88)
  Pallas kernels: 40.7 us -> 35.7 us
    pallas_call x1, Pallas kernels: 35.9 us -> 31 us  [shards(): pl.pallas_call(functools.partial(comm_kernel, sizes[0] * sizes[1] * sizes...]
where the time goes in v3:
time: 36.4 us; the launch traced here: 36.3 us
  Pallas kernels  35.7 us (98%)
  between operations  0.64 us (2%)
    pallas_call x1, Pallas kernels, shards(): pl.pallas_call(functools.partial(comm_kernel, sizes[0] * sizes[1] * sizes...  31 us
    pallas_call x1, Pallas kernels, shards(): pl.pallas_call(functools.partial(tv_kernel, sizes), out_shape=(result, re...  4.73 us

profile of v3, /device:TPU:1, one launch (start us, length us, event | category | flops | bytes accessed | tf_op | source)
XLA Modules:
  0.0 36.3 jit_solution(3277306470586434531)
XLA Ops:
  0.6 31.0 %decode_exchange.1 = (f32[22,24,128]{2,1,0:T(8,128)S(1)}, f32[2,24,128]{2,1,0:T(8,128)S(1)}, f32[2,24,128]{2,1,0:T(8,128)S(1)}, f32[16,16,128]{2,1,0:T(8,128)S(1)}) custom-call(f32[4,128,16,128]{3,2,1,0:T(8,128)} %partials.1, s32[32,128]{1,0:T(8,128)} %code_bits.1, s32[32]{0:T(128)} %group_map.1, f32[16,16,128]{2,1,0:T(8,128)} %velocity.1), custom_call_target="tpu_custom_call" | custom-call | tf_op jit(solution)/shard_map/decode_exchange/pallas_call | solution.py:478
  31.6 4.7 %tv_steps.1 = (f32[16,16,128]{2,1,0:T(8,128)}, f32[16,16,128]{2,1,0:T(8,128)}) custom-call(f32[22,24,128]{2,1,0:T(8,128)S(1)} %get-tuple-element.6.t_in, f32[2,24,128]{2,1,0:T(8,128)S(1)} %get-tuple-element.7.eh_in, f32[2,24,128]{2,1,0:T(8,128)S(1)} %get-tuple-element.8.el_in, f32[16,16,128]{2,1,0:T(8,128)S(1)} %get-tuple-element.9.g_in), custom_call_target="tpu_custom_call" | custom-call | tf_op jit(solution)/shard_map/tv_steps/pallas_call | solution.py:510
